TPU v7x, 32 devices: a whole 2x2x4 slice. The times are simulated.
32 devices in a mesh: dp: 4 (over z), row: 2 (over x), col: 4 (over y, core).
Axes of the slice: x: 2, y: 2, z: 4, core: 2. Of those that a mesh axis runs over, the one named last changes fastest.
Arguments:
- images: bfloat16 [32, 729, 1152], P(('dp', 'row', 'col')), may hold values from -6 to 6
- cotangent: bfloat16 [32, 729, 1152], P(('dp', 'row', 'col')), may hold values from -6 to 6
- first_gain: float32 [1152], replicated, may hold values from 0.25 to 1.75
- first_shift: float32 [1152], replicated, may hold values from -3 to 3
- query_weight: bfloat16 [1152, 1152], P('row', 'col'), may hold values from -0.1875 to 0.1875
- query_bias: float32 [1152], P('col'), may hold values from -3 to 3
- key_weight: bfloat16 [1152, 1152], P('row', 'col'), may hold values from -0.1875 to 0.1875
- value_weight: bfloat16 [1152, 1152], P('row', 'col'), may hold values from -0.1875 to 0.1875
- value_bias: float32 [1152], P('col'), may hold values from -3 to 3
- output_weight: bfloat16 [1152, 1152], P('col', 'row'), may hold values from -0.75 to 0.75
- output_bias: float32 [1152], replicated, may hold values from -3 to 3
- second_gain: float32 [1152], replicated, may hold values from 0.1 to 1.9
- second_shift: float32 [1152], replicated, may hold values from -3 to 3
- expand_weight: bfloat16 [1152, 4304], P('row', 'col'), may hold values from -0.1875 to 0.1875
- expand_bias: float32 [4304], P('col'), may hold values from -3 to 3
- shrink_weight: bfloat16 [4304, 1152], P('col', 'row'), may hold values from -0.1875 to 0.1875
- shrink_bias: float32 [1152], replicated, may hold values from -3 to 3
Outputs:
- layer_out: bfloat16 [32, 729, 1152], P(('dp', 'row', 'col'))
- grad_images: bfloat16 [32, 729, 1152], P(('dp', 'row', 'col'))
- grad_first_gain: float32 [1152], replicated
- grad_first_shift: float32 [1152], replicated
- grad_query_weight: float32 [1152, 1152], P('row', 'col')
- grad_query_bias: float32 [1152], P('col')
- grad_key_weight: float32 [1152, 1152], P('row', 'col')
- grad_value_weight: float32 [1152, 1152], P('row', 'col')
- grad_value_bias: float32 [1152], P('col')
- grad_output_weight: float32 [1152, 1152], P('col', 'row')
- grad_output_bias: float32 [1152], replicated
- grad_second_gain: float32 [1152], replicated
- grad_second_shift: float32 [1152], replicated
- grad_expand_weight: float32 [1152, 4304], P('row', 'col')
- grad_expand_bias: float32 [4304], P('col')
- grad_shrink_weight: float32 [4304, 1152], P('col', 'row')
- grad_shrink_bias: float32 [1152], replicated
All inputs are finite; a program needn't handle non-finite values.
Results may differ from a plain program's by a relative error of at most 0.038.
Values may be sent and summed in bfloat16 or wider, within the bound.
A program may use at most 448 MiB of HBM per device.

v0:
```python
import jax
import jax.numpy as jnp
from jax import lax
from jax.sharding import PartitionSpec as P

HEAD_DIM = 72
EPS = 1e-06
contract_last = (((2,), (1,)), ((), ()))
contract_rows = (((0, 1), (0, 1)), ((), ()))


def gelu_tanh(value):
    return jax.nn.gelu(value, approximate=True)


def norm_forward(stream, gain, shift):
    average = jnp.mean(stream, axis=-1, keepdims=True)
    second = jnp.mean(stream * stream, axis=-1, keepdims=True)
    inverse = lax.rsqrt(second - average * average + EPS)
    normed = (stream - average) * inverse
    return (normed, inverse, (normed * gain + shift).astype(jnp.bfloat16))


def norm_backward(grad_out, normed, inverse, gain):
    scaled = grad_out * gain
    first = jnp.mean(scaled, axis=-1, keepdims=True)
    second = jnp.mean(scaled * normed, axis=-1, keepdims=True)
    return inverse * (scaled - first - normed * second)


def spread(block):
    feature_part = lax.all_to_all(block, "row", split_axis=2, concat_axis=0, tiled=True)
    return lax.all_gather(feature_part, "col", axis=0, tiled=True)


def join_back(summed):
    return lax.all_to_all(
        summed.astype(jnp.bfloat16), "row", split_axis=0, concat_axis=2, tiled=True
    ).astype(summed.dtype)


def project_in(normed_bf, weight):
    gathered = spread(normed_bf)
    summed = lax.psum_scatter(
        jnp.dot(gathered, weight, preferred_element_type=jnp.float32).astype(jnp.bfloat16),
        "row",
        scatter_dimension=0,
        tiled=True,
    ).astype(jnp.float32)
    return (summed, gathered)


def project_out(block_bf, weight):
    partial_sums = jnp.dot(
        lax.all_gather(block_bf, "row", axis=0, tiled=True),
        weight,
        preferred_element_type=jnp.float32,
    )
    return join_back(
        lax.psum_scatter(
            partial_sums.astype(jnp.bfloat16), "col", scatter_dimension=0, tiled=True
        ).astype(jnp.float32)
    )


def back_out(grad_bf, acts_bf, weight):
    grads_all = spread(grad_bf)
    grad_acts = lax.psum_scatter(
        lax.dot_general(
            grads_all, weight, contract_last, preferred_element_type=jnp.float32
        ).astype(jnp.bfloat16),
        "row",
        scatter_dimension=0,
        tiled=True,
    ).astype(jnp.float32)
    grad_weight = lax.dot_general(
        lax.all_gather(acts_bf, "row", axis=0, tiled=True),
        grads_all,
        contract_rows,
        preferred_element_type=jnp.float32,
    )
    return (grad_acts, grad_weight)


def back_in(grad_bf, weight, normed_bf):
    inputs_all = spread(normed_bf)
    piece = lax.all_gather(grad_bf, "row", axis=0, tiled=True)
    contrib = lax.dot_general(piece, weight, contract_last, preferred_element_type=jnp.float32)
    partial_sums = contrib
    weight_grad = lax.dot_general(
        inputs_all, piece, contract_rows, preferred_element_type=jnp.float32
    )
    partial_sums, weight_grad = (partial_sums, weight_grad)
    grad_inputs = join_back(
        lax.psum_scatter(
            partial_sums.astype(jnp.bfloat16), "col", scatter_dimension=0, tiled=True
        ).astype(jnp.float32)
    )
    return (grad_inputs, weight_grad)


def split_heads(block):
    return block.reshape(block.shape[0], block.shape[1] // HEAD_DIM, HEAD_DIM)


def head_scores(queries, key_rows):
    scores = jnp.einsum(
        "qhd,khd->hqk",
        split_heads(queries),
        split_heads(key_rows),
        preferred_element_type=jnp.float32,
    )
    return scores * HEAD_DIM ** (-0.5)


def attend(queries, key_rows, value_rows):

    def one_image(triple):
        scores = head_scores(triple[0], triple[1])
        peak = jnp.max(scores, axis=-1, keepdims=True)
        log_total = peak + jnp.log(jnp.sum(jnp.exp(scores - peak), axis=-1, keepdims=True))
        attention = jnp.exp(scores - log_total).astype(jnp.bfloat16)
        mixed = jnp.einsum(
            "hqk,khd->qhd", attention, split_heads(triple[2]), preferred_element_type=jnp.float32
        )
        return (mixed.reshape(triple[0].shape).astype(jnp.bfloat16), log_total)

    return lax.map(one_image, (queries, key_rows, value_rows))


def attend_back(queries, key_rows, value_rows, attended, log_total, grad_attended):
    scale = HEAD_DIM ** (-0.5)

    def one_image(group):
        image_q, image_k, image_v, image_out, image_total, image_grad = group
        attention = jnp.exp(head_scores(image_q, image_k) - image_total)
        grad_heads = split_heads(image_grad)
        grad_probs = jnp.einsum(
            "qhd,khd->hqk", grad_heads, split_heads(image_v), preferred_element_type=jnp.float32
        )
        delta = jnp.einsum(
            "qhd,qhd->hq", grad_heads, split_heads(image_out), preferred_element_type=jnp.float32
        )[..., None]
        grad_scores = (attention * (grad_probs - delta)).astype(jnp.bfloat16)
        grad_queries = (
            jnp.einsum(
                "hqk,khd->qhd",
                grad_scores,
                split_heads(image_k),
                preferred_element_type=jnp.float32,
            )
            * scale
        )
        grad_keys = (
            jnp.einsum(
                "hqk,qhd->khd",
                grad_scores,
                split_heads(image_q),
                preferred_element_type=jnp.float32,
            )
            * scale
        )
        grad_values = jnp.einsum(
            "hqk,qhd->khd",
            attention.astype(jnp.bfloat16),
            grad_heads,
            preferred_element_type=jnp.float32,
        )
        shape = image_q.shape
        return (grad_queries.reshape(shape), grad_keys.reshape(shape), grad_values.reshape(shape))

    return lax.map(one_image, (queries, key_rows, value_rows, attended, log_total, grad_attended))


def feature_terms(grad_input1, normed1, grad_middle, grad_input2, normed2, grad_result):
    token_axes = (0, 1)
    return (
        jnp.sum(grad_input1 * normed1, axis=token_axes),
        jnp.sum(grad_input1, axis=token_axes),
        jnp.sum(grad_middle, axis=token_axes),
        jnp.sum(grad_input2 * normed2, axis=token_axes),
        jnp.sum(grad_input2, axis=token_axes),
        jnp.sum(grad_result, axis=token_axes),
    )


def embed_part(part_sum):
    start = lax.axis_index("col") * part_sum.shape[0]
    whole = jnp.zeros((part_sum.shape[0] * lax.axis_size("col"),), jnp.float32)
    return lax.dynamic_update_slice_in_dim(whole, part_sum, start, 0)


def grid_layer(images, cotangent, params):
    (
        first_gain,
        first_shift,
        query_weight,
        query_bias,
        key_weight,
        value_weight,
        value_bias,
        output_weight,
        output_bias,
        second_gain,
        second_shift,
        expand_weight,
        expand_bias,
        shrink_weight,
        shrink_bias,
    ) = params
    width = query_weight.shape[1]
    joined = jnp.concatenate((query_weight, key_weight, value_weight), axis=1)
    stream = images.astype(jnp.float32)
    normed1, inverse1, input1 = norm_forward(stream, first_gain, first_shift)
    projected, kept_first = project_in(input1, joined)
    queries = (projected[..., :width] + query_bias).astype(jnp.bfloat16)
    key_rows = projected[..., width : 2 * width].astype(jnp.bfloat16)
    value_rows = (projected[..., 2 * width :] + value_bias).astype(jnp.bfloat16)
    attended, log_total = attend(queries, key_rows, value_rows)
    middle = stream + project_out(attended, output_weight) + output_bias
    normed2, inverse2, input2 = norm_forward(middle, second_gain, second_shift)
    expanded, kept_second = project_in(input2, expand_weight)
    before = expanded + expand_bias
    hidden = gelu_tanh(before).astype(jnp.bfloat16)
    result = middle + project_out(hidden, shrink_weight) + shrink_bias
    grad_result = cotangent.astype(jnp.float32)
    grad_hidden, grad_shrink = back_out(cotangent, hidden, shrink_weight)
    gelu_back = jax.vjp(gelu_tanh, before)[1]
    grad_before = gelu_back(grad_hidden)[0]
    grad_input2, grad_expand = back_in(grad_before.astype(jnp.bfloat16), expand_weight, input2)
    grad_middle = grad_result + norm_backward(grad_input2, normed2, inverse2, second_gain)
    grad_attended, grad_output = back_out(grad_middle.astype(jnp.bfloat16), attended, output_weight)
    grad_queries, grad_keys, grad_values = attend_back(
        queries, key_rows, value_rows, attended, log_total, grad_attended.astype(jnp.bfloat16)
    )
    grad_joined_rows = jnp.concatenate((grad_queries, grad_keys, grad_values), axis=-1).astype(
        jnp.bfloat16
    )
    grad_input1, grad_joined = back_in(grad_joined_rows, joined, input1)
    grad_stream = grad_middle + norm_backward(grad_input1, normed1, inverse1, first_gain)
    token_axes = (0, 1)
    features = feature_terms(grad_input1, normed1, grad_middle, grad_input2, normed2, grad_result)
    biases = (
        embed_part(jnp.sum(grad_queries, axis=token_axes)),
        embed_part(jnp.sum(grad_values, axis=token_axes)),
        embed_part(jnp.sum(grad_before, axis=token_axes)),
    )
    blocks = (
        grad_joined[:, :width],
        grad_joined[:, width : 2 * width],
        grad_joined[:, 2 * width :],
        grad_output,
        grad_expand,
        grad_shrink,
    )
    return (result, grad_stream, features, biases, blocks)


def shards(
    images,
    cotangent,
    first_gain,
    first_shift,
    query_weight,
    query_bias,
    key_weight,
    value_weight,
    value_bias,
    output_weight,
    output_bias,
    second_gain,
    second_shift,
    expand_weight,
    expand_bias,
    shrink_weight,
    shrink_bias,
):
    params = (
        first_gain,
        first_shift,
        query_weight,
        query_bias,
        key_weight,
        value_weight,
        value_bias,
        output_weight,
        output_bias,
        second_gain,
        second_shift,
        expand_weight,
        expand_bias,
        shrink_weight,
        shrink_bias,
    )
    result, grad_stream, features, biases, blocks = grid_layer(images, cotangent, params)
    totals = lax.psum(
        (
            features[0],
            features[1],
            features[2],
            features[3],
            features[4],
            features[5],
            biases[0],
            biases[1],
            biases[2],
        ),
        ("dp", "row", "col"),
    )
    col_index = lax.axis_index("col")
    query_part = query_bias.shape[0]
    expand_part = expand_bias.shape[0]
    query_bias_grad = lax.dynamic_slice_in_dim(totals[6], col_index * query_part, query_part, 0)
    value_bias_grad = lax.dynamic_slice_in_dim(totals[7], col_index * query_part, query_part, 0)
    expand_bias_grad = lax.dynamic_slice_in_dim(totals[8], col_index * expand_part, expand_part, 0)
    weight_totals = (
        lax.psum(blocks[0].astype(jnp.bfloat16), "dp").astype(jnp.float32),
        lax.psum(blocks[1].astype(jnp.bfloat16), "dp").astype(jnp.float32),
        lax.psum(blocks[2].astype(jnp.bfloat16), "dp").astype(jnp.float32),
        lax.psum(blocks[3].astype(jnp.bfloat16), "dp").astype(jnp.float32),
        lax.psum(blocks[4].astype(jnp.bfloat16), "dp").astype(jnp.float32),
        lax.psum(blocks[5].astype(jnp.bfloat16), "dp").astype(jnp.float32),
    )
    return (
        result.astype(jnp.bfloat16),
        grad_stream.astype(jnp.bfloat16),
        totals[0],
        totals[1],
        weight_totals[0],
        query_bias_grad,
        weight_totals[1],
        weight_totals[2],
        value_bias_grad,
        weight_totals[3],
        totals[2],
        totals[3],
        totals[4],
        weight_totals[4],
        expand_bias_grad,
        weight_totals[5],
        totals[5],
    )


def solution(mesh):
    placed = (
        P(("dp", "row", "col"), None, None),
        P(("dp", "row", "col"), None, None),
        P(),
        P(),
        P("row", "col"),
        P("col"),
        P("row", "col"),
        P("row", "col"),
        P("col"),
        P("col", "row"),
        P(),
        P(),
        P(),
        P("row", "col"),
        P("col"),
        P("col", "row"),
        P(),
    )
    return jax.shard_map(
        shards,
        mesh=mesh,
        in_specs=placed,
        out_specs=(
            P(("dp", "row", "col"), None, None),
            P(("dp", "row", "col"), None, None),
            P(),
            P(),
            P("row", "col"),
            P("col"),
            P("row", "col"),
            P("row", "col"),
            P("col"),
            P("col", "row"),
            P(),
            P(),
            P(),
            P("row", "col"),
            P("col"),
            P("col", "row"),
            P(),
        ),
        check_vma=False,
    )
```

profile of v0, /device:TPU:0, one launch (start us, length us, event | category | flops | bytes accessed | tf_op | source)
XLA Modules:
  0.0 2109.9 jit_solution(17329852611036355849)
XLA Ops:
  12.2 7.6 copy.176
  20.3 11.7 reduce.14
  32.0 5.9 reshape.487
  37.9 25.5 %all_to_all.118 = bf16[2,2,209952]{2,1,0:T(2,128)(2,1)S(1)} all-to-all(bf16[2,2,209952]{2,1,0:T(2,128)(2,1)} %reshape.487), channel_id=1, replica_groups=mesh['dp'=4,'row'=2,'col'=4] {'row'}, dimensions={0} | all-to-all | bytes 3359232 | tf_op jit(solution)/shard_map/all_to_all | solution.py:32
  63.5 5.7 reshape.488
  74.0 50.2 %all-gather.21.cloned.1.call-done = bf16[8,1,729,576]{2,3,1,0:T(8,128)(2,1)} async-done(((bf16[2,1,729,576]{2,3,1,0:T(8,128)(2,1)}), bf16[8,1,729,576]{2,3,1,0:T(8,128)(2,1)}) %all-gather.21.cloned.1.call-update) | async-done | bytes 6718480 | tf_op jit(solution)/shard_map/all_gather | solution.py:33
  124.3 14.3 fusion.37
  138.8 122.5 %reduce-scatter.9.cloned.1.call-done = bf16[4,729,864]{2,1,0:T(8,128)(2,1)} async-done(((bf16[8,729,864]{2,1,0:T(8,128)(2,1)}), bf16[4,729,864]{2,1,0:T(8,128)(2,1)}) %reduce-scatter.9.cloned.1.call-update) | async-done | bytes 5038864 | tf_op jit(solution)/shard_map/reduce_scatter | solution.py:44
  261.4 4.4 slice.30
  275.4 4.1 copy.182
  283.5 32.8 %while.26 = (s32[]{:T(128)}, bf16[4,729,288]{1,2,0:T(8,128)(2,1)}, f32[4,4,729,1]{2,1,3,0:T(4,128)}, bf16[4,729,288]{1,2,0:T(8,128)(2,1)}, bf16[4,729,288]{1,2,0...) while((s32[]{:T(128)}, bf16[4,729,288]{1,2,0:T(8,128)(2,1)}, f32[4,4,729,1]{2,1,3,0:T(4,128)}, ...), condition=%wide.region_6.7_spmd, body=%wide.region_3.6_spmd.sunk | while | flops 629433152 | bytes 30664516 | solution.py:128
  316.6 49.3 %all-gather.13.cloned.1.call-done = bf16[8,729,288]{1,2,0:T(8,128)(2,1)} async-done(((bf16[4,729,288]{1,2,0:T(8,128)(2,1)}), bf16[8,729,288]{1,2,0:T(8,128)(2,1)}) %all-gather.13.cloned.1.call-update) | async-done | bytes 3359248 | tf_op jit(solution)/shard_map/all_gather | solution.py:55
  365.9 8.8 convolution_convert_fusion.5
  376.1 7.5 copy.188
  383.6 11.9 reduce.16
  395.6 5.9 reshape.489
  401.5 24.2 %all_to_all.119 = bf16[2,2,209952]{2,1,0:T(2,128)(2,1)S(1)} all-to-all(bf16[2,2,209952]{2,1,0:T(2,128)(2,1)} %reshape.489), channel_id=1, replica_groups=mesh['dp'=4,'row'=2,'col'=4] {'row'}, dimensions={0} | all-to-all | bytes 3359232 | tf_op jit(solution)/shard_map/all_to_all | solution.py:32
  425.6 5.6 reshape.490
  434.8 4.2 reduce-scatter.11.cloned.1.call-done
  439.0 25.5 %all_to_all.120 = bf16[2,729,576]{1,2,0:T(8,128)(2,1)S(1)} all-to-all(bf16[2,729,576]{1,2,0:T(8,128)(2,1)} %reduce-scatter.11.cloned.1.call-done), channel_id=1, replica_groups=mesh['dp'=4,'row'=2,'col'=4] {'row'}, dimensions={0} | all-to-all | bytes 3359232 | tf_op jit(solution)/shard_map/all_to_all | solution.py:37
  466.6 5.3 copy.184
  477.1 7.6 copy.185
  484.6 11.8 reduce.15
  496.4 5.9 reshape.491
  502.3 23.4 %all_to_all.121 = bf16[2,2,209952]{2,1,0:T(2,128)(2,1)S(1)} all-to-all(bf16[2,2,209952]{2,1,0:T(2,128)(2,1)} %reshape.491), channel_id=1, replica_groups=mesh['dp'=4,'row'=2,'col'=4] {'row'}, dimensions={0} | all-to-all | bytes 3359232 | tf_op jit(solution)/shard_map/all_to_all | solution.py:32
  525.7 5.7 reshape.492
  535.3 16.6 convolution_convert_fusion
  551.9 33.1 %all-gather.23.cloned.1.call-done = bf16[8,1,729,576]{2,3,1,0:T(8,128)(2,1)} async-done(((bf16[2,1,729,576]{2,3,1,0:T(8,128)(2,1)}), bf16[8,1,729,576]{2,3,1,0:T(8,128)(2,1)}) %all-gather.23.cloned.1.call-update) | async-done | bytes 6718480 | tf_op jit(solution)/shard_map/all_gather | solution.py:33
  585.1 16.6 convolution_convert_fusion.1
  601.7 137.7 %reduce-scatter.17.cloned.1.call-done = bf16[4,729,1076]{1,2,0:T(8,128)(2,1)} async-done(((bf16[8,729,1076]{1,2,0:T(8,128)(2,1)}), bf16[4,729,1076]{1,2,0:T(8,128)(2,1)}) %reduce-scatter.17.cloned.1.call-update) | async-done | bytes 6275248 | tf_op jit(solution)/shard_map/reduce_scatter | solution.py:68
  739.4 154.3 %reduce-scatter.13.cloned.1.call-done = bf16[4,729,1076]{1,2,0:T(8,128)(2,1)} async-done(((bf16[8,729,1076]{1,2,0:T(8,128)(2,1)}), bf16[4,729,1076]{1,2,0:T(8,128)(2,1)}) %reduce-scatter.13.cloned.1.call-update) | async-done | bytes 6275248 | tf_op jit(solution)/shard_map/reduce_scatter | solution.py:44
  893.7 17.1 fusion.91
  911.7 159.4 %all-gather.17.cloned.1.call-done = bf16[8,729,1076]{1,2,0:T(8,128)(2,1)} async-done(((bf16[4,729,1076]{1,2,0:T(8,128)(2,1)}), bf16[8,729,1076]{1,2,0:T(8,128)(2,1)}) %all-gather.17.cloned.1.call-update) | async-done | bytes 12550480 | tf_op jit(solution)/shard_map/all_gather | solution.py:87
  1071.0 15.9 convolution_convert_fusion.2
  1087.0 145.5 %all-gather.15.cloned.1.call-done = bf16[8,729,1076]{1,2,0:T(8,128)(2,1)} async-done(((bf16[4,729,1076]{1,2,0:T(8,128)(2,1)}), bf16[8,729,1076]{1,2,0:T(8,128)(2,1)}) %all-gather.15.cloned.1.call-update) | async-done | bytes 12550480 | tf_op jit(solution)/shard_map/all_gather | solution.py:55
  1232.5 15.9 convolution_convert_fusion.3
  1248.4 50.8 %reduce-scatter.19.cloned.1.call-done = bf16[2,729,576]{1,2,0:T(8,128)(2,1)} async-done(((bf16[8,729,576]{1,2,0:T(8,128)(2,1)}), bf16[2,729,576]{1,2,0:T(8,128)(2,1)}) %reduce-scatter.19.cloned.1.call-update) | async-done | bytes 1679632 | tf_op jit(solution)/shard_map/reduce_scatter | solution.py:95
  1303.1 62.8 %reduce-scatter.15.cloned.1.call-done = bf16[2,729,576]{1,2,0:T(8,128)(2,1)} async-done(((bf16[8,729,576]{1,2,0:T(8,128)(2,1)}), bf16[2,729,576]{1,2,0:T(8,128)(2,1)}) %reduce-scatter.15.cloned.1.call-update) | async-done | bytes 1679632 | tf_op jit(solution)/shard_map/reduce_scatter | solution.py:60
  1365.9 4.7 all-to-all-start.3
  1373.2 5.3 copy.190
  1385.0 7.1 all-to-all-done.3
  1395.6 5.2 copy.187
  1400.8 6.5 fusion.93
  1410.7 8.9 copy.191
  1419.6 11.9 reduce.17
  1431.5 6.2 reshape.493
  1437.7 23.0 %all_to_all.122 = bf16[2,2,209952]{2,1,0:T(2,128)(2,1)} all-to-all(bf16[2,2,209952]{2,1,0:T(2,128)(2,1)S(1)} %reshape.493), channel_id=1, replica_groups=mesh['dp'=4,'row'=2,'col'=4] {'row'}, dimensions={0} | all-to-all | bytes 3359232 | tf_op jit(solution)/shard_map/all_to_all | solution.py:32
  1460.6 5.6 reshape.494
  1468.0 49.9 %all-gather.27.cloned.1.call-done = bf16[8,1,729,576]{2,3,1,0:T(8,128)(2,1)} async-done(((bf16[2,1,729,576]{2,3,1,0:T(8,128)(2,1)}), bf16[8,1,729,576]{2,3,1,0:T(8,128)(2,1)}) %all-gather.27.cloned.1.call-update) | async-done | bytes 6718480 | tf_op jit(solution)/shard_map/all_gather | solution.py:33
  1517.9 7.7 fusion.71
  1525.7 47.8 %reduce-scatter.21.cloned.1.call-done = bf16[4,729,288]{1,2,0:T(8,128)(2,1)} async-done(((bf16[8,729,288]{1,2,0:T(8,128)(2,1)}), bf16[4,729,288]{1,2,0:T(8,128)(2,1)}) %reduce-scatter.21.cloned.1.call-update) | async-done | bytes 1679632 | tf_op jit(solution)/shard_map/reduce_scatter | solution.py:68
  1573.5 70.2 %while.27 = (s32[]{:T(128)}, f32[4,729,288]{1,2,0:T(8,128)}, bf16[4,729,288]{1,2,0:T(8,128)(2,1)}, f32[4,729,288]{1,2,0:T(8,128)S(1)}, bf16[4,729,288]{1,2,0:T(8...) while((s32[]{:T(128)}, f32[4,729,288]{1,2,0:T(8,128)}, ...), condition=%wide.region_18.19_spmd, body=%wide.region_17.18_spmd.sunk | while | flops 1549022848 | bytes 52812796 | solution.py:172
  1651.1 8.0 copy.196
  1659.2 130.3 %all-gather.19.cloned.1.call-done = bf16[8,729,864]{2,1,0:T(8,128)(2,1)} async-done(((bf16[4,729,864]{2,1,0:T(8,128)(2,1)}), bf16[8,729,864]{2,1,0:T(8,128)(2,1)}) %all-gather.19.cloned.1.call-update) | async-done | bytes 10077712 | tf_op jit(solution)/shard_map/all_gather | solution.py:87
  1789.5 13.6 convolution_convert_fusion.4
  1803.2 14.9 fusion.68
  1818.0 15.1 fusion.65
  1833.1 7.8 fusion.83
  1840.9 10.2 bitcast_convert_fusion
  1852.6 14.8 reduce-scatter.23.cloned.1.call-done
  1872.1 159.5 %all-reduce.4.cloned.1.call-done = (bf16[576,288]{1,0:T(8,128)(2,1)}, bf16[576,288]{1,0:T(8,128)(2,1)}, bf16[576,288]{1,0:T(8,128)(2,1)}, bf16[288,576]{1,0:T(8,...) async-done(((bf16[576,288]{1,0:T(8,128)(2,1)}, bf16[576,288]{1,0:T(8,128)(2,1)}, bf16[576,288]{1,0:T(8,128)(2,1)}, bf16[288,576]{1,0:T(8,128)(2,1)}, ...) | async-done | bytes 3806224 | tf_op jit(solution)/shard_map/psum | solution.py:317
  2046.6 5.3 copy.197
  2055.0 41.5 %all-reduce = (f32[1152]{0:T(1024)}, f32[1152]{0:T(1024)}, f32[1152]{0:T(1024)S(1)}, f32[1152]{0:T(1024)S(1)}, f32[1152]{0:T(1024)}, /*index=5*/f32[1152]{0:T(10...) all-reduce(f32[1152]{0:T(1024)S(1)} %get-tuple-element.309, ...), channel_id=1, replica_groups=mesh['dp'=4,'row'=2,'col'=4] {'dp','row','col'}, use_global_device_ids=true, to_apply=%region_23.24 | all-reduce | flops 13520 | bytes 108160 | tf_op jit(solution)/shard_map/psum | solution.py:296
  2098.5 4.5 fusion.55
  (268 shorter events, 199.3 us)
Async XLA Ops:
  7.2 577.9 %copy-start = (bf16[576,1076]{1,0:T(8,128)(2,1)S(1)}, bf16[576,1076]{1,0:T(8,128)(2,1)}, u32[]{:S(2)}) copy-start(bf16[576,1076]{1,0:T(8,128)(2,1)} %param.34) | copy-start | bytes 3718660
  7.2 117.1 %all-gather.21.cloned.1.call-start = ((), (), s32[]{:S(2)}) async-start(), calls=%async_computation.28 | async-start | bytes 8847360 | tf_op jit(solution)/shard_map/all_gather | solution.py:33
  9.4 0.6 copy-start.23
  9.4 0.6 copy-start.25
  69.1 4.1 copy-start.17
  69.1 4.4 copy-start.18
  69.1 4.7 copy-start.19
  72.7 188.6 %reduce-scatter.9.cloned.1.call-start = ((), (), s32[]{:S(2)}) async-start(), calls=%async_computation.16 | async-start | bytes 15826944 | tf_op jit(solution)/shard_map/reduce_scatter | solution.py:44
  73.5 65.0 %copy-start.11 = (bf16[576,288]{1,0:T(8,128)(2,1)}, bf16[576,288]{1,0:T(8,128)(2,1)S(1)}, u32[]{:S(2)}) copy-start(bf16[576,288]{1,0:T(8,128)(2,1)S(1)} %copy.178) | copy-start | bytes 995332
  73.8 64.8 %copy-start.13 = (bf16[576,288]{1,0:T(8,128)(2,1)}, bf16[576,288]{1,0:T(8,128)(2,1)S(1)}, u32[]{:S(2)}) copy-start(bf16[576,288]{1,0:T(8,128)(2,1)S(1)} %copy.179) | copy-start | bytes 995332
  74.0 64.5 %copy-start.15 = (bf16[576,288]{1,0:T(8,128)(2,1)}, bf16[576,288]{1,0:T(8,128)(2,1)S(1)}, u32[]{:S(2)}) copy-start(bf16[576,288]{1,0:T(8,128)(2,1)S(1)} %copy.180) | copy-start | bytes 995332
  138.6 227.3 %all-gather.13.cloned.1.call-start = ((), (), s32[]{:S(2)}) async-start(), calls=%async_computation.17 | async-start | bytes 5308416 | tf_op jit(solution)/shard_map/all_gather | solution.py:55
  268.7 3.2 copy-start.36
  268.7 3.2 copy-start.37
  283.5 82.4 %copy-start.39 = (bf16[288,576]{1,0:T(8,128)(2,1)S(1)}, bf16[288,576]{1,0:T(8,128)(2,1)}, u32[]{:S(2)}) copy-start(bf16[288,576]{1,0:T(8,128)(2,1)} %param.30) | copy-start | bytes 995332
  316.3 58.4 %copy-start.6 = (bf16[4,729,288]{1,2,0:T(8,128)(2,1)}, bf16[4,729,288]{1,2,0:T(8,128)(2,1)S(1)}, u32[]{:S(2)}) copy-start(bf16[4,729,288]{1,2,0:T(8,128)(2,1)S(1)} %get-tuple-element.600) | copy-start | bytes 5038852
  316.3 122.7 %reduce-scatter.11.cloned.1.call-start = ((), (), s32[]{:S(2)}) async-start(), calls=%async_computation.18 | async-start | bytes 8847360 | tf_op jit(solution)/shard_map/reduce_scatter | solution.py:60
  374.7 1.5 copy-start.8
  374.7 160.6 %all-gather.25.cloned.1.call-start = ((), (), s32[]{:S(2)}) async-start(), calls=%async_computation.30 | async-start | bytes 8847360 | tf_op jit(solution)/shard_map/all_gather | solution.py:33
  434.8 150.3 %all-gather.23.cloned.1.call-start = ((), (), s32[]{:S(2)}) async-start(), calls=%async_computation.29 | async-start | bytes 8847360 | tf_op jit(solution)/shard_map/all_gather | solution.py:33
  466.6 5.3 copy-start.4
  466.6 5.3 copy-start.32
  472.0 4.5 copy-start.21
  472.0 4.5 copy-start.33
  474.7 1.8 copy-start.2
  531.4 3.9 copy-start.38
  535.0 204.4 %reduce-scatter.17.cloned.1.call-start = ((), (), s32[]{:S(2)}) async-start(), calls=%async_computation.22 | async-start | bytes 19906560 | tf_op jit(solution)/shard_map/reduce_scatter | solution.py:68
  551.9 341.8 %reduce-scatter.13.cloned.1.call-start = ((), (), s32[]{:S(2)}) async-start(), calls=%async_computation.19 | async-start | bytes 19906560 | tf_op jit(solution)/shard_map/reduce_scatter | solution.py:44
  601.6 292.0 %copy-start.34 = (f32[1076]{0:T(1024)S(1)}, f32[1076]{0:T(1024)}, u32[]{:S(2)}) copy-start(f32[1076]{0:T(1024)} %param.35) | copy-start | bytes 12916
  601.7 469.4 %all-gather.17.cloned.1.call-start = ((), (), s32[]{:S(2)}) async-start(), calls=%async_computation.23 | async-start | bytes 19906560 | tf_op jit(solution)/shard_map/all_gather | solution.py:87
  910.8 321.7 %all-gather.15.cloned.1.call-start = ((), (), s32[]{:S(2)}) async-start(), calls=%async_computation.20 | async-start | bytes 19906560 | tf_op jit(solution)/shard_map/all_gather | solution.py:55
  911.4 387.9 %reduce-scatter.19.cloned.1.call-start = ((), (), s32[]{:S(2)}) async-start(), calls=%async_computation.24 | async-start | bytes 8847360 | tf_op jit(solution)/shard_map/reduce_scatter | solution.py:95
  1086.9 279.0 %reduce-scatter.15.cloned.1.call-start = ((), (), s32[]{:S(2)}) async-start(), calls=%async_computation.21 | async-start | bytes 8847360 | tf_op jit(solution)/shard_map/reduce_scatter | solution.py:60
  1299.3 66.6 %all-to-all-start.5 = ((bf16[2,729,576]{1,2,0:T(8,128)(2,1)}), bf16[2,729,576]{1,2,0:T(8,128)(2,1)S(1)}, u32[]{:S(2)}, u32[]{:S(2)}) async-start(bf16[2,729,576]{1,2,0:T(8,128)(2,1)} %reduce-scatter.19.cloned.1.call-done), calls=%async_computation.11 | async-start | bytes 3538944 | tf_op jit(solution)/shard_map/all_to_all | solution.py:37
  1365.9 7.2 copy-start.7
  1365.9 26.2 %all-to-all-start.3 = ((bf16[2,729,576]{1,2,0:T(8,128)(2,1)}), bf16[2,729,576]{1,2,0:T(8,128)(2,1)}, u32[]{:S(2)}, u32[]{:S(2)}) async-start(bf16[2,729,576]{1,2,0:T(8,128)(2,1)} %reduce-scatter.15.cloned.1.call-done), calls=%async_computation.7 | async-start | bytes 3538944 | tf_op jit(solution)/shard_map/all_to_all | solution.py:37
  1370.6 147.3 %all-gather.27.cloned.1.call-start = ((), (), s32[]{:S(2)}) async-start(), calls=%async_computation.31 | async-start | bytes 8847360 | tf_op jit(solution)/shard_map/all_gather | solution.py:33
  1373.1 8.3 copy-start.3
  1395.6 5.2 copy-start.35
  1467.8 105.7 %reduce-scatter.21.cloned.1.call-start = ((), (), s32[]{:S(2)}) async-start(), calls=%async_computation.25 | async-start | bytes 5308416 | tf_op jit(solution)/shard_map/reduce_scatter | solution.py:68
  1525.6 263.9 %all-gather.19.cloned.1.call-start = ((), (), s32[]{:S(2)}) async-start(), calls=%async_computation.26 | async-start | bytes 15826944 | tf_op jit(solution)/shard_map/all_gather | solution.py:87
  1643.7 3.9 copy-start.9
  1659.1 130.4 %copy-start.12 = (bf16[576,288]{1,0:T(8,128)(2,1)S(1)}, bf16[576,288]{1,0:T(8,128)(2,1)}, u32[]{:S(2)}) copy-start(bf16[576,288]{1,0:T(8,128)(2,1)} %copy-done.11) | copy-start | bytes 995332
  1659.1 130.4 %copy-start.14 = (bf16[576,288]{1,0:T(8,128)(2,1)S(1)}, bf16[576,288]{1,0:T(8,128)(2,1)}, u32[]{:S(2)}) copy-start(bf16[576,288]{1,0:T(8,128)(2,1)} %copy-done.13) | copy-start | bytes 995332
  1659.1 130.4 %copy-start.16 = (bf16[576,288]{1,0:T(8,128)(2,1)S(1)}, bf16[576,288]{1,0:T(8,128)(2,1)}, u32[]{:S(2)}) copy-start(bf16[576,288]{1,0:T(8,128)(2,1)} %copy-done.15) | copy-start | bytes 995332
  1659.1 208.3 %reduce-scatter.23.cloned.1.call-start = ((), (), s32[]{:S(2)}) async-start(), calls=%async_computation.27 | async-start | bytes 8847360 | tf_op jit(solution)/shard_map/reduce_scatter | solution.py:95
  1803.1 228.5 %all-reduce.4.cloned.1.call-start = ((), (), s32[]{:S(2)}) async-start(), calls=%async_computation.32 | async-start | bytes 8699904 | tf_op jit(solution)/shard_map/psum | solution.py:317
  1803.1 37.8 %slice-start = ((s8[10551296]{0:T(1024)(128)(4,1)}), s8[4194304]{0:T(1024)(128)(4,1)S(1)}, s32[]{:S(2)}) async-start(s8[10551296]{0:T(1024)(128)(4,1)} %bitcast.269), calls=%async_computation.33 | async-start | bytes 8388608
  1803.1 37.8 %slice-start.1 = ((s8[10551296]{0:T(1024)(128)(4,1)}), s8[4194304]{0:T(1024)(128)(4,1)S(1)}, s32[]{:S(2)}) async-start(s8[10551296]{0:T(1024)(128)(4,1)} %bitcast.269), calls=%async_computation.34 | async-start | bytes 8388608
  1818.0 22.9 %slice-start.2 = ((s8[10551296]{0:T(1024)(128)(4,1)}), s8[2162688]{0:T(1024)(128)(4,1)S(1)}, s32[]{:S(2)}) async-start(s8[10551296]{0:T(1024)(128)(4,1)} %bitcast.269), calls=%async_computation.35 | async-start | bytes 4325376
  1852.6 18.6 copy-start.22
  1852.6 18.7 copy-start.27
  1852.6 19.0 copy-start.31
  1867.4 176.1 %all-to-all-start.7 = ((bf16[2,729,576]{1,2,0:T(8,128)(2,1)}), bf16[2,729,576]{1,2,0:T(8,128)(2,1)S(1)}, u32[]{:S(2)}, u32[]{:S(2)}) async-start(bf16[2,729,576]{1,2,0:T(8,128)(2,1)} %reduce-scatter.23.cloned.1.call-done), calls=%async_computation.15 | async-start | bytes 3538944 | tf_op jit(solution)/shard_map/all_to_all | solution.py:37
  2031.6 6.3 copy-start.20
  2033.7 8.1 copy-start.10
  2046.6 5.3 copy-start.5
  2046.6 5.3 copy-start.24
  2046.6 5.3 copy-start.26
  2051.9 3.1 copy-start.28
  2051.9 3.1 copy-start.29
  2051.9 3.1 copy-start.30
  2097.8 5.2 copy-start.1
Sparse Core Ops, SparseCore 0:
  72.9 51.3 all-gather.20
  138.7 122.6 reduce-scatter.8
  316.5 49.3 all-gather.12
  374.8 64.1 reduce-scatter.10
  440.5 50.8 all-gather.24
  535.1 49.8 all-gather.22
  587.4 151.9 reduce-scatter.16
  741.7 151.9 reduce-scatter.12
  910.9 160.0 all-gather.16
  1072.4 160.0 all-gather.14
  1235.0 64.1 reduce-scatter.18
  1301.7 64.1 reduce-scatter.14
  1467.9 49.9 all-gather.26
  1525.7 47.7 reduce-scatter.20
  1659.2 130.1 all-gather.18
  1803.2 64.1 reduce-scatter.22
  1871.3 160.2 all-reduce.3
where the time goes:
time: 2120 us; the launch traced here: 2110 us
  waiting for transfers between devices  1380 us (65%)
  matrix products  208 us (10%)
  local copies, waits for them, and re-layouts  194 us (9%)
  blocking collectives  163 us (8%)
  other arithmetic  135 us (6%)
    all_gather x2, waiting for transfers between devices, back_in(): piece = lax.all_gather(grad_bf, 'row', axis=0, tiled=True)  290 us
    reduce_scatter x2, waiting for transfers between devices, project_in(): lax.psum_scatter(jnp.dot(gathered, weight, preferred_element_type=jnp.flo...  277 us
    all_gather x2, waiting for transfers between devices, project_out(): lax.all_gather(block_bf, 'row', axis=0, tiled=True)  195 us
    reduce_scatter x2, waiting for transfers between devices, back_out(): lax.psum_scatter(lax.dot_general(grads_all, weight, contract_last, prefer...  185 us
    psum x1, waiting for transfers between devices, shards(): lax.psum(blocks[0].astype(jnp.bfloat16), 'dp').astype(jnp.float32)  159 us
    all_gather x4, waiting for transfers between devices, spread(): return lax.all_gather(feature_part, 'col', axis=0, tiled=True)  133 us
    all_to_all x4, blocking collectives, spread(): lax.all_to_all(block, 'row', split_axis=2, concat_axis=0, tiled=True)  96.1 us
    unnamed x106, local copies, waits for them, and re-layouts  77.6 us
  transfers between devices with their start and end apart: 20, of which 17 were waited for; matrix products, arithmetic and copies ran while one was open for 11% of the time, Pallas kernels for 0%

commit v1 on v0

--- a/solution.py
+++ b/solution.py
@@ -29,7 +29,10 @@
 
 
 def spread(block):
-    feature_part = lax.all_to_all(block, "row", split_axis=2, concat_axis=0, tiled=True)
+    feature_part = jnp.concatenate(
+        lax.all_to_all(jnp.stack(jnp.split(block, lax.axis_size("row"), axis=2)), "row", 0, 0),
+        axis=0,
+    )
     return lax.all_gather(feature_part, "col", axis=0, tiled=True)
 
 

time: 2120 us -> 2000 us (0.943)
  local copies, waits for them, and re-layouts: 194 us -> 103 us
  other arithmetic: 135 us -> 73.1 us
  waiting for transfers between devices: 1380 us -> 1410 us
    unnamed x106 -> x98, local copies, waits for them, and re-layouts: 77.6 us -> 28.2 us
    unnamed x5 -> x1, other arithmetic: 47.3 us -> 0.01 us
    convert_element_type x7 -> x0, local copies, waits for them, and re-layouts: 45.2 us -> none  [the longest x4 21.1 us: join_back(): return lax.all_to_all(summed.astype(jnp.bfloat16), 'row', split_axis=0, c...]
    reduce_scatter x2, waiting for transfers between devices: 67 us -> 95.1 us  [project_out(): lax.psum_scatter(partial_sums.astype(jnp.bfloat16), 'col', scatter_dimens...]
  transfers between devices with their start and end apart: 20 -> 20, of which waited for: 17 -> 17; matrix products, arithmetic and copies ran while one was open for 11% -> 7% of each run, Pallas kernels for 0% -> 0%
where the time goes in v1:
time: 2000 us; the launch traced here: 1990 us
  waiting for transfers between devices  1410 us (70%)
  matrix products  208 us (10%)
  blocking collectives  166 us (8%)
  local copies, waits for them, and re-layouts  103 us (5%)
  other arithmetic  73.1 us (4%)
    all_gather x2, waiting for transfers between devices, back_in(): piece = lax.all_gather(grad_bf, 'row', axis=0, tiled=True)  290 us
    reduce_scatter x2, waiting for transfers between devices, project_in(): lax.psum_scatter(jnp.dot(gathered, weight, preferred_element_type=jnp.flo...  277 us
    all_gather x2, waiting for transfers between devices, project_out(): lax.all_gather(block_bf, 'row', axis=0, tiled=True)  194 us
    reduce_scatter x2, waiting for transfers between devices, back_out(): lax.psum_scatter(lax.dot_general(grads_all, weight, contract_last, prefer...  185 us
    psum x1, waiting for transfers between devices, shards(): lax.psum(blocks[0].astype(jnp.bfloat16), 'dp').astype(jnp.float32)  156 us
    all_gather x4, waiting for transfers between devices, spread(): return lax.all_gather(feature_part, 'col', axis=0, tiled=True)  131 us
    all_to_all x4, blocking collectives, spread(): lax.all_to_all(jnp.stack(jnp.split(block, lax.axis_size('row'), axis=2)),...  99.2 us
    reduce_scatter x2, waiting for transfers between devices, project_out(): lax.psum_scatter(partial_sums.astype(jnp.bfloat16), 'col', scatter_dimens...  95.1 us
  transfers between devices with their start and end apart: 20, of which 17 were waited for; matrix products, arithmetic and copies ran while one was open for 7% of the time, Pallas kernels for 0%

profile of v1, /device:TPU:0, one launch (start us, length us, event | category | flops | bytes accessed | tf_op | source)
XLA Modules:
  0.0 1990.5 jit_solution(3591952807556114953)
XLA Ops:
  7.3 2.7 copy.104
  12.1 26.2 %all_to_all.58 = bf16[2,1,729,576]{2,3,1,0:T(8,128)(2,1)} all-to-all(bf16[2,1,729,576]{2,3,1,0:T(8,128)(2,1)S(1)} %pad_maximum_fusion.1), channel_id=1, replica_groups=mesh['dp'=4,'row'=2,'col'=4] {'row'}, dimensions={0} | all-to-all | bytes 3359232 | tf_op jit(solution)/shard_map/all_to_all | solution.py:33
  43.7 46.2 %all-gather.21.cloned.1.call-done = bf16[8,1,729,576]{2,3,1,0:T(8,128)(2,1)} async-done(((bf16[2,1,729,576]{2,3,1,0:T(8,128)(2,1)}), bf16[8,1,729,576]{2,3,1,0:T(8,128)(2,1)}) %all-gather.21.cloned.1.call-update) | async-done | bytes 6718480 | tf_op jit(solution)/shard_map/all_gather | solution.py:36
  89.9 14.6 fusion.37
  105.1 122.2 %reduce-scatter.9.cloned.1.call-done = bf16[4,729,864]{2,1,0:T(8,128)(2,1)} async-done(((bf16[8,729,864]{2,1,0:T(8,128)(2,1)}), bf16[4,729,864]{2,1,0:T(8,128)(2,1)}) %reduce-scatter.9.cloned.1.call-update) | async-done | bytes 5038864 | tf_op jit(solution)/shard_map/reduce_scatter | solution.py:47
  227.3 4.4 slice.30
  231.7 4.1 copy.110
  235.8 3.2 convert_element_type.244
  239.0 3.4 fusion.40
  242.4 4.1 copy.109
  246.5 4.0 copy.108
  250.5 33.4 %while.26 = (s32[]{:T(128)}, bf16[4,729,288]{1,2,0:T(8,128)(2,1)}, f32[4,4,729,1]{2,1,3,0:T(4,128)}, bf16[4,729,288]{1,2,0:T(8,128)(2,1)}, bf16[4,729,288]{1,2,0...) while((s32[]{:T(128)}, bf16[4,729,288]{1,2,0:T(8,128)(2,1)}, f32[4,4,729,1]{2,1,3,0:T(4,128)}, ...), condition=%wide.region_6.7_spmd, body=%wide.region_3.6_spmd.sunk | while | flops 629433152 | bytes 30664516 | solution.py:131
  284.1 49.3 %all-gather.13.cloned.1.call-done = bf16[8,729,288]{1,2,0:T(8,128)(2,1)} async-done(((bf16[4,729,288]{1,2,0:T(8,128)(2,1)}), bf16[8,729,288]{1,2,0:T(8,128)(2,1)}) %all-gather.13.cloned.1.call-update) | async-done | bytes 3359248 | tf_op jit(solution)/shard_map/all_gather | solution.py:58
  333.4 8.8 convolution_convert_fusion.5
  342.3 3.8 copy.111
  347.8 24.8 %all_to_all.59 = bf16[2,1,729,576]{2,3,1,0:T(8,128)(2,1)} all-to-all(bf16[2,1,729,576]{2,3,1,0:T(8,128)(2,1)S(1)} %pad_maximum_fusion.3), channel_id=1, replica_groups=mesh['dp'=4,'row'=2,'col'=4] {'row'}, dimensions={0} | all-to-all | bytes 3359232 | tf_op jit(solution)/shard_map/all_to_all | solution.py:33
  372.7 33.9 %reduce-scatter.11.cloned.1.call-done = bf16[2,729,576]{1,2,0:T(8,128)(2,1)} async-done(((bf16[8,729,576]{1,2,0:T(8,128)(2,1)}), bf16[2,729,576]{1,2,0:T(8,128)(2,1)}) %reduce-scatter.11.cloned.1.call-update) | async-done | bytes 1679632 | tf_op jit(solution)/shard_map/reduce_scatter | solution.py:63
  406.6 25.1 %all_to_all.60 = bf16[2,729,576]{1,2,0:T(8,128)(2,1)S(1)} all-to-all(bf16[2,729,576]{1,2,0:T(8,128)(2,1)} %reduce-scatter.11.cloned.1.call-done), channel_id=1, replica_groups=mesh['dp'=4,'row'=2,'col'=4] {'row'}, dimensions={0} | all-to-all | bytes 3359232 | tf_op jit(solution)/shard_map/all_to_all | solution.py:40
  435.1 24.2 %all_to_all.61 = bf16[2,1,729,576]{2,3,1,0:T(8,128)(2,1)} all-to-all(bf16[2,1,729,576]{2,3,1,0:T(8,128)(2,1)S(1)} %pad_maximum_fusion.2), channel_id=1, replica_groups=mesh['dp'=4,'row'=2,'col'=4] {'row'}, dimensions={0} | all-to-all | bytes 3359232 | tf_op jit(solution)/shard_map/all_to_all | solution.py:33
  459.4 16.6 convolution_convert_fusion
  476.3 34.9 %all-gather.23.cloned.1.call-done = bf16[8,1,729,576]{2,3,1,0:T(8,128)(2,1)} async-done(((bf16[2,1,729,576]{2,3,1,0:T(8,128)(2,1)}), bf16[8,1,729,576]{2,3,1,0:T(8,128)(2,1)}) %all-gather.23.cloned.1.call-update) | async-done | bytes 6718480 | tf_op jit(solution)/shard_map/all_gather | solution.py:36
  511.2 16.6 convolution_convert_fusion.1
  527.8 137.6 %reduce-scatter.17.cloned.1.call-done = bf16[4,729,1076]{1,2,0:T(8,128)(2,1)} async-done(((bf16[8,729,1076]{1,2,0:T(8,128)(2,1)}), bf16[4,729,1076]{1,2,0:T(8,128)(2,1)}) %reduce-scatter.17.cloned.1.call-update) | async-done | bytes 6275248 | tf_op jit(solution)/shard_map/reduce_scatter | solution.py:71
  665.5 154.3 %reduce-scatter.13.cloned.1.call-done = bf16[4,729,1076]{1,2,0:T(8,128)(2,1)} async-done(((bf16[8,729,1076]{1,2,0:T(8,128)(2,1)}), bf16[4,729,1076]{1,2,0:T(8,128)(2,1)}) %reduce-scatter.13.cloned.1.call-update) | async-done | bytes 6275248 | tf_op jit(solution)/shard_map/reduce_scatter | solution.py:47
  819.8 17.1 fusion.104
  837.5 159.6 %all-gather.17.cloned.1.call-done = bf16[8,729,1076]{1,2,0:T(8,128)(2,1)} async-done(((bf16[4,729,1076]{1,2,0:T(8,128)(2,1)}), bf16[8,729,1076]{1,2,0:T(8,128)(2,1)}) %all-gather.17.cloned.1.call-update) | async-done | bytes 12550480 | tf_op jit(solution)/shard_map/all_gather | solution.py:90
  997.1 15.9 convolution_convert_fusion.2
  1013.4 145.1 %all-gather.15.cloned.1.call-done = bf16[8,729,1076]{1,2,0:T(8,128)(2,1)} async-done(((bf16[4,729,1076]{1,2,0:T(8,128)(2,1)}), bf16[8,729,1076]{1,2,0:T(8,128)(2,1)}) %all-gather.15.cloned.1.call-update) | async-done | bytes 12550480 | tf_op jit(solution)/shard_map/all_gather | solution.py:58
  1158.5 15.9 convolution_convert_fusion.3
  1174.5 50.8 %reduce-scatter.19.cloned.1.call-done = bf16[2,729,576]{1,2,0:T(8,128)(2,1)} async-done(((bf16[8,729,576]{1,2,0:T(8,128)(2,1)}), bf16[2,729,576]{1,2,0:T(8,128)(2,1)}) %reduce-scatter.19.cloned.1.call-update) | async-done | bytes 1679632 | tf_op jit(solution)/shard_map/reduce_scatter | solution.py:98
  1225.3 4.7 all-to-all-start.5
  1230.7 61.2 %reduce-scatter.15.cloned.1.call-done = bf16[2,729,576]{1,2,0:T(8,128)(2,1)} async-done(((bf16[8,729,576]{1,2,0:T(8,128)(2,1)}), bf16[2,729,576]{1,2,0:T(8,128)(2,1)}) %reduce-scatter.15.cloned.1.call-update) | async-done | bytes 1679632 | tf_op jit(solution)/shard_map/reduce_scatter | solution.py:63
  1291.9 4.7 all-to-all-start.3
  1296.7 2.9 fusion.60
  1300.2 3.4 fusion.67
  1304.2 13.9 all-to-all-done.3
  1320.2 5.1 fusion.106
  1327.5 24.0 %all_to_all.62 = bf16[2,1,729,576]{2,3,1,0:T(8,128)(2,1)} all-to-all(bf16[2,1,729,576]{2,3,1,0:T(8,128)(2,1)S(1)} %pad_maximum_fusion.4), channel_id=1, replica_groups=mesh['dp'=4,'row'=2,'col'=4] {'row'}, dimensions={0} | all-to-all | bytes 3359232 | tf_op jit(solution)/shard_map/all_to_all | solution.py:33
  1351.6 50.0 %all-gather.27.cloned.1.call-done = bf16[8,1,729,576]{2,3,1,0:T(8,128)(2,1)} async-done(((bf16[2,1,729,576]{2,3,1,0:T(8,128)(2,1)}), bf16[8,1,729,576]{2,3,1,0:T(8,128)(2,1)}) %all-gather.27.cloned.1.call-update) | async-done | bytes 6718480 | tf_op jit(solution)/shard_map/all_gather | solution.py:36
  1401.6 7.4 fusion.84
  1409.3 47.6 %reduce-scatter.21.cloned.1.call-done = bf16[4,729,288]{1,2,0:T(8,128)(2,1)} async-done(((bf16[8,729,288]{1,2,0:T(8,128)(2,1)}), bf16[4,729,288]{1,2,0:T(8,128)(2,1)}) %reduce-scatter.21.cloned.1.call-update) | async-done | bytes 1679632 | tf_op jit(solution)/shard_map/reduce_scatter | solution.py:71
  1457.0 70.3 %while.27 = (s32[]{:T(128)}, f32[4,729,288]{1,2,0:T(8,128)}, bf16[4,729,288]{1,2,0:T(8,128)(2,1)}, f32[4,729,288]{1,2,0:T(8,128)S(1)}, bf16[4,729,288]{1,2,0:T(8...) while((s32[]{:T(128)}, f32[4,729,288]{1,2,0:T(8,128)}, ...), condition=%wide.region_18.19_spmd, body=%wide.region_17.18_spmd.sunk | while | flops 1549022848 | bytes 52812796 | solution.py:175
  1464.5 2.6 fusion.164
  1467.1 3.2 multiply_convert_fusion.3
  1484.7 3.2 multiply_convert_fusion.3
  1502.3 3.2 multiply_convert_fusion.3
  1517.2 2.6 fusion.164
  1519.8 3.2 multiply_convert_fusion.3
  1527.2 3.9 fusion.108
  1531.2 3.4 pad_maximum_fusion
  1534.6 7.8 copy.117
  1542.4 130.3 %all-gather.19.cloned.1.call-done = bf16[8,729,864]{2,1,0:T(8,128)(2,1)} async-done(((bf16[4,729,864]{2,1,0:T(8,128)(2,1)}), bf16[8,729,864]{2,1,0:T(8,128)(2,1)}) %all-gather.19.cloned.1.call-update) | async-done | bytes 10077712 | tf_op jit(solution)/shard_map/all_gather | solution.py:90
  1672.7 13.7 convolution_convert_fusion.4
  1686.7 14.8 fusion.81
  1701.5 15.1 fusion.78
  1716.6 7.8 fusion.96
  1724.4 10.2 bitcast_convert_fusion
  1736.1 14.7 reduce-scatter.23.cloned.1.call-done
  1750.8 4.7 all-to-all-start.7
  1758.9 156.0 %all-reduce.4.cloned.1.call-done = (bf16[576,288]{1,0:T(8,128)(2,1)}, bf16[576,288]{1,0:T(8,128)(2,1)}, bf16[576,288]{1,0:T(8,128)(2,1)}, bf16[288,576]{1,0:T(8,...) async-done(((bf16[576,288]{1,0:T(8,128)(2,1)}, bf16[576,288]{1,0:T(8,128)(2,1)}, bf16[576,288]{1,0:T(8,128)(2,1)}, bf16[288,576]{1,0:T(8,128)(2,1)}, ...) | async-done | bytes 3806224 | tf_op jit(solution)/shard_map/psum | solution.py:320
  1928.1 2.9 fusion.54
  1931.0 41.5 %all-reduce = (f32[1152]{0:T(1024)}, f32[1152]{0:T(1024)}, f32[1152]{0:T(1024)S(1)}, f32[1152]{0:T(1024)S(1)}, f32[1152]{0:T(1024)}, /*index=5*/f32[1152]{0:T(10...) all-reduce(f32[1152]{0:T(1024)S(1)} %get-tuple-element.243, ...), channel_id=1, replica_groups=mesh['dp'=4,'row'=2,'col'=4] {'dp','row','col'}, use_global_device_ids=true, to_apply=%region_23.24 | all-reduce | flops 13520 | bytes 108160 | tf_op jit(solution)/shard_map/psum | solution.py:299
  1973.8 5.1 fusion.53
  1979.0 3.8 copy.119
  (255 shorter events, 127.1 us)
Async XLA Ops:
  7.2 504.0 %copy-start = (bf16[576,1076]{1,0:T(8,128)(2,1)S(1)}, bf16[576,1076]{1,0:T(8,128)(2,1)}, u32[]{:S(2)}) copy-start(bf16[576,1076]{1,0:T(8,128)(2,1)} %param.34) | copy-start | bytes 3718660
  7.2 4.0 copy-start.18
  7.2 3.9 copy-start.31
  7.2 82.7 %all-gather.21.cloned.1.call-start = ((), (), s32[]{:S(2)}) async-start(), calls=%async_computation.28 | async-start | bytes 8847360 | tf_op jit(solution)/shard_map/all_gather | solution.py:36
  10.0 422.0 %copy-start.2 = (bf16[1,729,1152]{1,2,0:T(8,128)(2,1)}, bf16[1,729,1152]{1,2,0:T(8,128)(2,1)S(1)}, u32[]{:S(2)}) copy-start(bf16[1,729,1152]{1,2,0:T(8,128)(2,1)S(1)} %copy.104) | copy-start | bytes 5038852
  10.5 0.6 copy-start.20
  10.6 0.6 copy-start.22
  38.3 188.9 %reduce-scatter.9.cloned.1.call-start = ((), (), s32[]{:S(2)}) async-start(), calls=%async_computation.16 | async-start | bytes 15826944 | tf_op jit(solution)/shard_map/reduce_scatter | solution.py:47
  39.6 64.8 %copy-start.12 = (bf16[576,288]{1,0:T(8,128)(2,1)}, bf16[576,288]{1,0:T(8,128)(2,1)S(1)}, u32[]{:S(2)}) copy-start(bf16[576,288]{1,0:T(8,128)(2,1)S(1)} %copy.105) | copy-start | bytes 995332
  104.5 228.9 %all-gather.13.cloned.1.call-start = ((), (), s32[]{:S(2)}) async-start(), calls=%async_computation.17 | async-start | bytes 5308416 | tf_op jit(solution)/shard_map/all_gather | solution.py:58
  235.8 3.2 copy-start.36
  235.8 3.2 copy-start.37
  250.5 82.9 %copy-start.39 = (bf16[288,576]{1,0:T(8,128)(2,1)S(1)}, bf16[288,576]{1,0:T(8,128)(2,1)}, u32[]{:S(2)}) copy-start(bf16[288,576]{1,0:T(8,128)(2,1)} %param.30) | copy-start | bytes 995332
  283.9 122.7 %reduce-scatter.11.cloned.1.call-start = ((), (), s32[]{:S(2)}) async-start(), calls=%async_computation.18 | async-start | bytes 8847360 | tf_op jit(solution)/shard_map/reduce_scatter | solution.py:63
  342.2 117.1 %all-gather.25.cloned.1.call-start = ((), (), s32[]{:S(2)}) async-start(), calls=%async_computation.30 | async-start | bytes 8847360 | tf_op jit(solution)/shard_map/all_gather | solution.py:36
  372.6 138.5 %all-gather.23.cloned.1.call-start = ((), (), s32[]{:S(2)}) async-start(), calls=%async_computation.29 | async-start | bytes 8847360 | tf_op jit(solution)/shard_map/all_gather | solution.py:36
  431.7 0.7 copy-start.35
  432.4 0.8 copy-start.17
  432.4 0.8 copy-start.32
  433.2 1.7 copy-start.4
  435.1 24.3 %copy-start.38 = (bf16[1076,576]{0,1:T(8,128)(2,1)S(1)}, bf16[1076,576]{0,1:T(8,128)(2,1)}, u32[]{:S(2)}) copy-start(bf16[1076,576]{0,1:T(8,128)(2,1)} %param.36) | copy-start | bytes 3718660
  459.3 206.1 %reduce-scatter.17.cloned.1.call-start = ((), (), s32[]{:S(2)}) async-start(), calls=%async_computation.22 | async-start | bytes 19906560 | tf_op jit(solution)/shard_map/reduce_scatter | solution.py:71
  476.0 343.7 %reduce-scatter.13.cloned.1.call-start = ((), (), s32[]{:S(2)}) async-start(), calls=%async_computation.19 | async-start | bytes 19906560 | tf_op jit(solution)/shard_map/reduce_scatter | solution.py:47
  527.7 292.0 %copy-start.33 = (f32[1076]{0:T(1024)S(1)}, f32[1076]{0:T(1024)}, u32[]{:S(2)}) copy-start(f32[1076]{0:T(1024)} %param.35) | copy-start | bytes 12916
  527.8 469.3 %all-gather.17.cloned.1.call-start = ((), (), s32[]{:S(2)}) async-start(), calls=%async_computation.23 | async-start | bytes 19906560 | tf_op jit(solution)/shard_map/all_gather | solution.py:90
  836.8 321.7 %all-gather.15.cloned.1.call-start = ((), (), s32[]{:S(2)}) async-start(), calls=%async_computation.20 | async-start | bytes 19906560 | tf_op jit(solution)/shard_map/all_gather | solution.py:58
  837.4 387.9 %reduce-scatter.19.cloned.1.call-start = ((), (), s32[]{:S(2)}) async-start(), calls=%async_computation.24 | async-start | bytes 8847360 | tf_op jit(solution)/shard_map/reduce_scatter | solution.py:98
  1013.0 279.0 %reduce-scatter.15.cloned.1.call-start = ((), (), s32[]{:S(2)}) async-start(), calls=%async_computation.21 | async-start | bytes 8847360 | tf_op jit(solution)/shard_map/reduce_scatter | solution.py:63
  1225.3 66.6 %all-to-all-start.5 = ((bf16[2,729,576]{1,2,0:T(8,128)(2,1)}), bf16[2,729,576]{1,2,0:T(8,128)(2,1)}, u32[]{:S(2)}, u32[]{:S(2)}) async-start(bf16[2,729,576]{1,2,0:T(8,128)(2,1)} %reduce-scatter.19.cloned.1.call-done), calls=%async_computation.11 | async-start | bytes 3538944 | tf_op jit(solution)/shard_map/all_to_all | solution.py:40
  1230.0 70.2 %copy-start.5 = (f32[1,729,1152]{1,2,0:T(8,128)S(1)}, f32[1,729,1152]{1,2,0:T(8,128)}, u32[]{:S(2)}) copy-start(f32[1,729,1152]{1,2,0:T(8,128)} %copy-done.4) | copy-start | bytes 10077700
  1291.9 26.2 %all-to-all-start.3 = ((bf16[2,729,576]{1,2,0:T(8,128)(2,1)}), bf16[2,729,576]{1,2,0:T(8,128)(2,1)}, u32[]{:S(2)}, u32[]{:S(2)}) async-start(bf16[2,729,576]{1,2,0:T(8,128)(2,1)} %reduce-scatter.15.cloned.1.call-done), calls=%async_computation.7 | async-start | bytes 3538944 | tf_op jit(solution)/shard_map/all_to_all | solution.py:40
  1296.7 105.0 %all-gather.27.cloned.1.call-start = ((), (), s32[]{:S(2)}) async-start(), calls=%async_computation.31 | async-start | bytes 8847360 | tf_op jit(solution)/shard_map/all_gather | solution.py:36
  1318.2 2.0 copy-start.7
  1318.2 2.0 copy-start.29
  1318.2 2.0 copy-start.30
  1318.2 2.0 copy-start.34
  1325.2 1.7 copy-start.6
  1327.5 74.2 %copy-start.40 = (bf16[288,576]{1,0:T(8,128)(2,1)S(1)}, bf16[288,576]{1,0:T(8,128)(2,1)}, u32[]{:S(2)}) copy-start(bf16[288,576]{1,0:T(8,128)(2,1)} %param.30) | copy-start | bytes 995332
  1351.5 105.4 %reduce-scatter.21.cloned.1.call-start = ((), (), s32[]{:S(2)}) async-start(), calls=%async_computation.25 | async-start | bytes 5308416 | tf_op jit(solution)/shard_map/reduce_scatter | solution.py:71
  1409.1 263.7 %all-gather.19.cloned.1.call-start = ((), (), s32[]{:S(2)}) async-start(), calls=%async_computation.26 | async-start | bytes 15826944 | tf_op jit(solution)/shard_map/all_gather | solution.py:90
  1527.2 3.9 copy-start.9
  1542.3 130.4 %copy-start.13 = (bf16[576,288]{1,0:T(8,128)(2,1)S(1)}, bf16[576,288]{1,0:T(8,128)(2,1)}, u32[]{:S(2)}) copy-start(bf16[576,288]{1,0:T(8,128)(2,1)} %copy-done.12) | copy-start | bytes 995332
  1542.3 130.4 %copy-start.14 = (bf16[576,288]{1,0:T(8,128)(2,1)S(1)}, bf16[576,288]{1,0:T(8,128)(2,1)}, u32[]{:S(2)}) copy-start(bf16[576,288]{1,0:T(8,128)(2,1)} %copy.106) | copy-start | bytes 995332
  1542.3 130.4 %copy-start.15 = (bf16[576,288]{1,0:T(8,128)(2,1)S(1)}, bf16[576,288]{1,0:T(8,128)(2,1)}, u32[]{:S(2)}) copy-start(bf16[576,288]{1,0:T(8,128)(2,1)} %copy.107) | copy-start | bytes 995332
  1542.4 208.4 %reduce-scatter.23.cloned.1.call-start = ((), (), s32[]{:S(2)}) async-start(), calls=%async_computation.27 | async-start | bytes 8847360 | tf_op jit(solution)/shard_map/reduce_scatter | solution.py:98
  1686.4 228.5 %all-reduce.4.cloned.1.call-start = ((), (), s32[]{:S(2)}) async-start(), calls=%async_computation.32 | async-start | bytes 8699904 | tf_op jit(solution)/shard_map/psum | solution.py:320
  1686.7 37.7 %slice-start = ((s8[10551296]{0:T(1024)(128)(4,1)}), s8[4194304]{0:T(1024)(128)(4,1)S(1)}, s32[]{:S(2)}) async-start(s8[10551296]{0:T(1024)(128)(4,1)} %bitcast.284), calls=%async_computation.33 | async-start | bytes 8388608
  1686.7 37.7 %slice-start.1 = ((s8[10551296]{0:T(1024)(128)(4,1)}), s8[4194304]{0:T(1024)(128)(4,1)S(1)}, s32[]{:S(2)}) async-start(s8[10551296]{0:T(1024)(128)(4,1)} %bitcast.284), calls=%async_computation.34 | async-start | bytes 8388608
  1701.5 22.8 %slice-start.2 = ((s8[10551296]{0:T(1024)(128)(4,1)}), s8[2162688]{0:T(1024)(128)(4,1)S(1)}, s32[]{:S(2)}) async-start(s8[10551296]{0:T(1024)(128)(4,1)} %bitcast.284), calls=%async_computation.35 | async-start | bytes 4325376
  1736.0 19.4 copy-start.19
  1736.1 19.5 copy-start.24
  1736.1 20.1 %copy-start.28 = (f32[2,576]{1,0:T(2,128)S(1)}, f32[2,576]{1,0:T(2,128)}, u32[]{:S(2)}) copy-start(f32[2,576]{1,0:T(2,128)} %get-tuple-element.247) | copy-start | bytes 13828
  1736.1 20.2 %copy-start.8 = (bf16[1,729,1152]{1,2,0:T(8,128)(2,1)S(1)}, bf16[1,729,1152]{1,2,0:T(8,128)(2,1)}, u32[]{:S(2)}) copy-start(bf16[1,729,1152]{1,2,0:T(8,128)(2,1)} %get-tuple-element.320) | copy-start | bytes 5038852
  1750.8 174.9 %all-to-all-start.7 = ((bf16[2,729,576]{1,2,0:T(8,128)(2,1)}), bf16[2,729,576]{1,2,0:T(8,128)(2,1)}, u32[]{:S(2)}, u32[]{:S(2)}) async-start(bf16[2,729,576]{1,2,0:T(8,128)(2,1)} %reduce-scatter.23.cloned.1.call-done), calls=%async_computation.15 | async-start | bytes 3538944 | tf_op jit(solution)/shard_map/all_to_all | solution.py:40
  1914.9 6.4 copy-start.16
  1914.9 7.3 copy-start.11
  1917.1 6.8 copy-start.10
  1923.9 4.2 copy-start.3
  1923.9 4.2 copy-start.21
  1923.9 4.2 copy-start.23
  1925.6 5.4 copy-start.25
  1925.6 5.4 copy-start.26
  1925.6 5.4 copy-start.27
  1973.8 9.6 copy-start.1
Sparse Core Ops, SparseCore 0:
  38.5 51.3 all-gather.20
  104.6 122.6 reduce-scatter.8
  284.0 49.3 all-gather.12
  342.4 64.1 reduce-scatter.10
  408.0 50.8 all-gather.24
  460.3 50.8 all-gather.22
  513.5 151.9 reduce-scatter.16
  667.8 151.9 reduce-scatter.12
  837.0 160.0 all-gather.16
  998.5 160.0 all-gather.14
  1161.1 64.1 reduce-scatter.18
  1227.7 64.1 reduce-scatter.14
  1351.7 49.9 all-gather.26
  1409.2 47.7 reduce-scatter.20
  1542.5 130.1 all-gather.18
  1686.5 64.1 reduce-scatter.22
  1754.6 160.2 all-reduce.3
